TPU v7x, 32 devices: a whole 2x2x4 slice. The times are simulated.
32 devices in a mesh: groups: 2 (over y), heads: 4 (over z), batch: 4 (over x, core).
Axes of the slice: x: 2, y: 2, z: 4, core: 2. Of those that a mesh axis runs over, the one named last changes fastest.
Arguments:
- queries: bfloat16 [128, 8192], P(('groups', 'batch'), 'heads'), parts along dimension 0, may hold values from -110 to 110
- new_kv: bfloat16 [16, 64, 256], P(('groups', 'heads'), 'batch'), parts along dimension 0, may hold values from -15 to 15
- kv_pool: bfloat16 [16, 192, 128, 256], P(('groups', 'heads'), 'batch'), parts along dimension 0, may hold values from -6 to 6
- page_counts: int32 [8, 16], P(('groups', 'batch')), parts along dimension 0, may hold values from 1 to 6, 48 in all within a row
- last_fill: int32 [8, 16], P(('groups', 'batch')), parts along dimension 0, may hold values from 1 to 128
- page_order: int32 [8, 48], P(('groups', 'batch')), parts along dimension 0, may hold values from 0 to 47, each once within a row
- hidden: bfloat16 [128, 8192], P(('groups', 'batch')), parts along dimension 0, may hold values from -0.59765625 to 0.59765625
- out_weight: bfloat16 [8192, 8192], P('heads'), may hold values from -0.5 to 0.5
- norm_gain: bfloat16 [8192], replicated, may hold values from 0.099609375 to 1.8984375
- sectioned: bfloat16 [8, 4, 8, 128, 256], P(('groups', 'heads'), 'batch'), parts along dimension 0, may hold values from -6 to 6
- routes: int32 [8, 4, 8, 1], P(('groups', 'heads'), 'batch'), parts along dimension 0, may hold values from 0 to 7; in each aligned block of 8 rows (0 to 7, 8 to 15, ..., all dimensions but the last counted through in order) at most 2 rows name the same one
Outputs:
- residual_out: bfloat16 [128, 8192], P(('groups', 'batch')), parts along dimension 0
- normed: bfloat16 [128, 8192], P(('groups', 'batch')), parts along dimension 0
- arrival: bfloat16 [16, 4, 4, 2, 128, 256], P(('groups', 'heads'), 'batch'), parts along dimension 0
There are 2 independent parts, one for each index of `groups`. A program takes and returns all parts, laid end to end along the dimension named above; an argument that names none is the same for every part. Nothing has to cross between parts.
Inputs may be any that keep to these rules, and one draw needn't show every extreme that they name: `routes`: every key-value head is named by at most 2 sectioned pages of one device. `page_counts`: the page counts of one batch owner sum to 48.
All inputs are finite; a program needn't handle non-finite values.
Results may differ from a plain program's by a relative error of at most 0.0066.
Values may be sent and summed in bfloat16 or wider, within the bound.
A program may use at most 128 MiB of HBM per device.

v0:
```python
import jax
import jax.numpy as jnp
from jax import lax
from jax.sharding import PartitionSpec as P

KV_HEADS = 8
PER_HEAD_CAP = 2
norm_epsilon = 1e-06


def attend(queries, new_kv, kv_pool, counts, fill, order):
    slot_count, pool_pages, page_size, lane_width = kv_pool.shape
    head_dim = lane_width // 2
    requests = queries.shape[0]
    score_scale = 1.0 / head_dim**0.5
    position = jnp.arange(pool_pages, dtype=jnp.int32)
    position_in_order = jnp.sum(
        jnp.where(order[None, :] == position[:, None], position[None, :], 0), axis=1
    )
    count_ends = jnp.cumsum(counts)
    starts = count_ends - counts
    owner_index = jnp.sum(
        (count_ends[None, :] <= position_in_order[:, None]).astype(jnp.int32), axis=1
    )
    member = owner_index[:, None] == jnp.arange(requests, dtype=jnp.int32)[None, :]
    member_float = member.astype(jnp.float32)
    within = position_in_order - jnp.sum(jnp.where(member, starts[None, :], 0), axis=1)
    context = (counts - 1) * page_size + fill
    context_limit = jnp.sum(jnp.where(member, context[None, :], 0), axis=1)
    live_tokens = (
        within[:, None] * page_size + jnp.arange(page_size, dtype=jnp.int32)[None, :]
        < context_limit[:, None]
    )
    page_queries = jnp.einsum(
        "pr,rlgd->lpgd", member.astype(jnp.bfloat16), queries, preferred_element_type=jnp.float32
    ).astype(jnp.bfloat16)
    scores = (
        jnp.einsum(
            "lpgd,lptd->lpgt",
            page_queries,
            kv_pool[..., :head_dim],
            preferred_element_type=jnp.float32,
        )
        * score_scale
    )
    scores = jnp.where(live_tokens[None, :, None, :], scores, -1e30)
    page_top = jnp.max(scores, axis=3)
    fresh_score = (
        jnp.einsum(
            "rlgd,lrd->lrg", queries, new_kv[..., :head_dim], preferred_element_type=jnp.float32
        )
        * score_scale
    )
    masked_top = jnp.where(member.T[None, :, :, None], page_top[:, None, :, :], -1e30)
    request_top = jnp.maximum(fresh_score, jnp.max(masked_top, axis=2))
    page_ref = jnp.einsum("pr,lrg->lpg", member_float, request_top, precision=lax.Precision.HIGHEST)
    weight = jnp.where(live_tokens[None, :, None, :], jnp.exp(scores - page_ref[..., None]), 0.0)
    page_den = jnp.sum(weight, axis=3)
    page_num = jnp.einsum(
        "lpgt,lptd->lpgd",
        weight.astype(jnp.bfloat16),
        kv_pool[..., head_dim:],
        preferred_element_type=jnp.float32,
    )
    fresh_weight = jnp.exp(fresh_score - request_top)
    fresh_rounded = lax.optimization_barrier(fresh_weight.astype(jnp.bfloat16)).astype(jnp.float32)
    denominator = (
        jnp.einsum("pr,lpg->lrg", member_float, page_den, precision=lax.Precision.HIGHEST)
        + fresh_weight
    )
    numerator = jnp.einsum("pr,lpgd->lrgd", member_float, page_num, precision=lax.Precision.HIGHEST)
    numerator = numerator + fresh_rounded[..., None] * new_kv[:, :, None, head_dim:].astype(
        jnp.float32
    )
    attended = numerator / denominator[..., None]
    attended = jnp.transpose(attended, (1, 0, 2, 3)).astype(jnp.bfloat16)
    return attended.reshape(requests, -1)


def landing_table(destination, head_total, most_pages):
    sectioned_count = destination.shape[0]
    order_ids = jnp.arange(sectioned_count, dtype=jnp.int32)
    same_head = destination[:, None] == destination[None, :]
    earlier = order_ids[:, None] > order_ids[None, :]
    page_rank = jnp.sum((same_head & earlier).astype(jnp.int32), axis=1)
    matches = (
        destination[None, None, :] == jnp.arange(head_total, dtype=jnp.int32)[:, None, None]
    ) & (page_rank[None, None, :] == jnp.arange(most_pages, dtype=jnp.int32)[None, :, None])
    source_index = jnp.sum(jnp.where(matches, order_ids[None, None, :], 0), axis=2)
    source_valid = jnp.any(matches, axis=2)
    return (source_index, source_valid)


def per_device(
    queries,
    new_kv,
    kv_pool,
    page_counts,
    last_fill,
    page_order,
    hidden,
    out_weight,
    norm_gain,
    sectioned,
    routes,
):
    head_count = lax.axis_size("heads")
    slots_dev = new_kv.shape[0]
    head_dim = kv_pool.shape[3] // 2
    requests = hidden.shape[0]
    group_size = queries.shape[1] // (slots_dev * head_dim)
    page_data = sectioned[0, 0]
    source_index, source_valid = landing_table(routes[0, 0, :, 0], KV_HEADS, PER_HEAD_CAP)
    cache_total = head_count * slots_dev
    target = (
        (
            jnp.arange(head_count, dtype=jnp.int32)[None, :] * slots_dev
            + jnp.arange(slots_dev, dtype=jnp.int32)[:, None]
        )
        * KV_HEADS
        // cache_total
    )
    picked = source_index[target]
    present = source_valid[target]
    outgoing = page_data[picked]
    outgoing = jnp.where(present[..., None, None], outgoing, jnp.zeros_like(outgoing))
    landed = lax.all_to_all(outgoing, "heads", split_axis=1, concat_axis=1, tiled=True)
    arrival = landed[:, None]
    query_block = queries.reshape(requests, slots_dev, group_size, head_dim)
    attn = attend(query_block, new_kv, kv_pool, page_counts[0], last_fill[0], page_order[0])
    partial_terms = jnp.dot(attn, out_weight, preferred_element_type=jnp.float32)
    summed = lax.psum(partial_terms, "heads")
    mixed = hidden.astype(jnp.float32) + summed
    mean_square = jnp.mean(mixed * mixed, axis=1, keepdims=True)
    normed = (mixed * lax.rsqrt(mean_square + norm_epsilon) * norm_gain.astype(jnp.float32)).astype(
        jnp.bfloat16
    )
    residual_out = mixed.astype(jnp.bfloat16)
    return (residual_out, normed, arrival)


def solution(mesh):
    return jax.shard_map(
        per_device,
        mesh=mesh,
        in_specs=(
            P(("groups", "batch"), "heads"),
            P(("groups", "heads"), "batch", None),
            P(("groups", "heads"), "batch", None, None),
            P(("groups", "batch"), None),
            P(("groups", "batch"), None),
            P(("groups", "batch"), None),
            P(("groups", "batch"), None),
            P("heads", None),
            P(),
            P(("groups", "heads"), "batch", None, None, None),
            P(("groups", "heads"), "batch", None, None),
        ),
        out_specs=(
            P(("groups", "batch"), None),
            P(("groups", "batch"), None),
            P(("groups", "heads"), "batch", None, None, None, None),
        ),
        check_vma=False,
    )
```

profile of v0, /device:TPU:0, one launch (start us, length us, event | category | flops | bytes accessed | tf_op | source)
XLA Modules:
  0.0 96.6 jit_solution(1213633889777169506)
XLA Ops:
  7.2 0.0 copy-start
  7.2 0.0 all-reduce.2.cloned.1.call-start
  7.2 0.8 select_reduce_fusion.1
  8.0 0.7 copy.69
  8.8 0.1 reduce
  8.9 0.1 convert_reduce_fusion
  9.0 0.7 add_bitcast_fusion
  9.7 0.1 select_reduce_fusion.3
  9.8 0.7 convert_bitcast_fusion
  10.5 0.8 copy.93
  11.4 0.3 fusion.10
  11.6 0.1 fusion.27
  11.8 0.1 copy.90
  11.9 0.1 add_compare_fusion
  12.0 3.7 %fusion.48 = (f32[2,48,8]{2,1,0:T(8,128)S(1)}, f32[2,48,8,128]{3,2,1,0:T(8,128)S(1)}) fusion(bf16[2,48,128,256]{3,2,1,0:T(8,128)(2,1)} %param.13, bf16[2,48,8,128]{3,1,2,0:T(8,128)(2,1)S(1)} %fusion.10, pred[48,128]{1,0:T(8,128)(4,1)S(1)} %add_compare_fusion), kind=kOutput, calls=%fused_computation.86 | convolution fusion | flops 25459968 | bytes 3744768 | tf_op jit(solution)/shard_map/lpgd,lptd->lpgt/dot_general | solution.py:38
  15.7 0.1 copy.72
  15.7 0.1 select_reduce_fusion
  15.9 0.1 copy.73
  15.9 0.1 convolution_bitcast_fusion.1
  16.1 0.1 copy.74
  16.2 0.3 fusion.15
  16.5 2.9 %fusion = f32[2,48,8,128]{3,2,1,0:T(8,128)S(1)} fusion(bf16[2,48,128,256]{3,2,1,0:T(8,128)(2,1)} %param.13, f32[2,48,8,128]{3,2,1,0:T(8,128)S(1)} %get-tuple-element.24, f32[2,48,8]{2,1,0:T(8,128)S(1)} %copy.74, pred[48,128]{1,0:T(8,128)(4,1)S(1)} %add_compare_fusion), kind=kOutput, calls=%fused_computation.3 | convolution fusion | flops 25460736 | bytes 3941376 | tf_op jit(solution)/shard_map/lpgt,lptd->lpgd/dot_general | solution.py:59
  19.3 0.1 copy.76
  19.4 0.1 fusion.13
  19.6 0.3 fusion.12
  19.9 0.0 copy-start.3
  19.9 13.7 %fusion.23 = f32[16,8192]{1,0:T(8,128)} fusion(bf16[2048,8192]{1,0:T(8,128)(2,1)} %param.18, bf16[2,8,16,128]{3,2,1,0:T(8,128)(2,1)S(1)} %bitcast.73), kind=kOutput, calls=%fused_computation.31 | convolution fusion | flops 536870912 | bytes 34144256 | tf_op jit(solution)/shard_map/dot_general | solution.py:131
  33.6 0.0 all-reduce.2.cloned.1.call-update
  33.6 0.2 convert_reduce_fusion.1
  33.8 0.1 and_reduce_fusion
  34.0 0.2 fusion.30
  34.2 0.1 reshape.257
  34.2 0.1 copy.79
  34.3 0.1 copy.82
  34.4 0.6 gather_fusion.1
  35.0 0.6 gather_fusion
  35.6 0.1 copy.92
  35.7 0.1 copy.84
  35.8 0.1 reshape.273
  35.9 0.6 gather_fusion.2
  36.5 0.1 broadcast_select_fusion
  36.6 1.1 %copy.85 = bf16[2,4,2,128,256]{4,3,2,0,1:T(8,128)(2,1)} copy(bf16[2,4,2,128,256]{4,3,2,1,0:T(8,128)(2,1)S(1)} %broadcast_select_fusion) | data formatting | bytes 2097152 | tf_op jit(solution)/shard_map/jit(_where)/select_n | solution.py:126
  37.7 6.3 %all-to-all-start = ((bf16[2,4,2,128,256]{4,3,2,0,1:T(8,128)(2,1)}), bf16[2,4,2,128,256]{4,3,2,0,1:T(8,128)(2,1)S(1)}, u32[]{:S(2)}, u32[]{:S(2)}) async-start(bf16[2,4,2,128,256]{4,3,2,0,1:T(8,128)(2,1)} %copy.85), calls=%async_computation | async-start | bytes 2097152 | tf_op jit(solution)/shard_map/all_to_all | solution.py:127
  44.1 41.5 %all-reduce.2.cloned.1.call-done = f32[16,8192]{1,0:T(8,128)} async-done(((f32[16,8192]{1,0:T(8,128)}), f32[16,8192]{1,0:T(8,128)}) %all-reduce.2.cloned.1.call-update) | async-done | bytes 524304 | tf_op jit(solution)/shard_map/psum | solution.py:132
  85.6 1.2 %multiply_reduce_fusion = f32[16]{0:T(128)S(1)} fusion(f32[16,8192]{1,0:T(8,128)} %all-reduce.2.cloned.1.call-done, bf16[16,8192]{1,0:T(8,128)(2,1)S(1)} %copy-done.1), kind=kLoop, calls=%fused_computation.19 | loop fusion | flops 524272 | bytes 786496 | tf_op jit(solution)/shard_map/reduce_sum | solution.py:134
  86.8 1.9 %multiply_convert_fusion = (bf16[16,8192]{1,0:T(8,128)(2,1)}, bf16[16,8192]{1,0:T(8,128)(2,1)}) fusion(f32[8192]{0:T(1024)S(1)} %convert_element_type.46, f32[16]{0:T(128)S(1)} %add_rsqrt_fusion, f32[16,8192]{1,0:T(8,128)} %all-reduce.2.cloned.1.call-done, bf16[16,8192]{1,0:T(8,128)(2,1)S(1)} %copy-done.1), kind=kLoop, calls=%fused_computation.18 | loop fusion | flops 786432 | bytes 1343552 | tf_op jit(solution)/shard_map/convert_element_type | solution.py:135
  88.7 0.0 all-to-all-done
  88.7 1.0 %copy.86 = bf16[2,1,4,2,128,256]{5,4,3,2,1,0:T(8,128)(2,1)} copy(bf16[2,1,4,2,128,256]{5,4,3,0,2,1:T(8,128)(2,1)S(1)} %bitcast.71) | data formatting | bytes 2097152
  (21 shorter events, 0.2 us)
Async XLA Ops:
  7.2 28.7 %copy-start = (bf16[1,1,8,128,256]{4,3,2,1,0:T(8,128)(2,1)S(1)}, bf16[1,1,8,128,256]{4,3,2,1,0:T(8,128)(2,1)}, u32[]{:S(2)}) copy-start(bf16[1,1,8,128,256]{4,3,2,1,0:T(8,128)(2,1)} %param.20) | copy-start | bytes 1572868
  7.2 78.4 %all-reduce.2.cloned.1.call-start = ((), (), s32[]{:S(2)}) async-start(), calls=%async_computation.1 | async-start | bytes 1048576 | tf_op jit(solution)/shard_map/psum | solution.py:132
  19.9 13.7 %copy-start.3 = (s32[1,1,8,1]{2,3,1,0:T(1,128)S(1)}, s32[1,1,8,1]{2,3,1,0:T(1,128)}, u32[]{:S(2)}) copy-start(s32[1,1,8,1]{2,3,1,0:T(1,128)} %param.21) | copy-start | bytes 100
  33.6 10.5 %copy-start.2 = (bf16[8192]{0:T(1024)(128)(2,1)S(1)}, bf16[8192]{0:T(1024)(128)(2,1)}, u32[]{:S(2)}) copy-start(bf16[8192]{0:T(1024)(128)(2,1)} %param.19) | copy-start | bytes 49156
  33.6 52.0 %copy-start.1 = (bf16[16,8192]{1,0:T(8,128)(2,1)S(1)}, bf16[16,8192]{1,0:T(8,128)(2,1)}, u32[]{:S(2)}) copy-start(bf16[16,8192]{1,0:T(8,128)(2,1)} %param.17) | copy-start | bytes 786436
  37.7 51.0 %all-to-all-start = ((bf16[2,4,2,128,256]{4,3,2,0,1:T(8,128)(2,1)}), bf16[2,4,2,128,256]{4,3,2,0,1:T(8,128)(2,1)S(1)}, u32[]{:S(2)}, u32[]{:S(2)}) async-start(bf16[2,4,2,128,256]{4,3,2,0,1:T(8,128)(2,1)} %copy.85), calls=%async_computation | async-start | bytes 2097152 | tf_op jit(solution)/shard_map/all_to_all | solution.py:127
Sparse Core Ops, SparseCore 0:
  33.7 51.7 all-reduce.1
where the time goes:
time: 97.1 us; the launch traced here: 96.6 us
  waiting for transfers between devices  41.5 us (43%)
  matrix products  21.2 us (22%)
  between operations  14.2 us (15%)
  other arithmetic  6.9 us (7%)
  local copies, waits for them, and re-layouts  6.39 us (7%)
  starting transfers between devices  6.38 us (7%)
    psum x1, waiting for transfers between devices, per_device(): summed = lax.psum(partial_terms, 'heads')  41.5 us
    dot_general x1, matrix products, per_device(): jnp.dot(attn, out_weight, preferred_element_type=jnp.float32)  13.7 us
    all_to_all x1, starting transfers between devices, per_device(): lax.all_to_all(outgoing, 'heads', split_axis=1, concat_axis=1, tiled=True)  6.35 us
    dot_general x1, matrix products, attend(): jnp.einsum('lpgd,lptd->lpgt', page_queries, kv_pool[..., :head_dim], pref...  3.69 us
    dot_general x1, matrix products, attend(): jnp.einsum('lpgt,lptd->lpgd', weight.astype(jnp.bfloat16), kv_pool[..., h...  2.86 us
  transfers between devices with their start and end apart: 2, of which 1 were waited for; matrix products, arithmetic and copies ran while one was open for 7% of the time, Pallas kernels for 0%

commit v1 on v0

--- a/solution.py
+++ b/solution.py
@@ -129,7 +129,9 @@
     query_block = queries.reshape(requests, slots_dev, group_size, head_dim)
     attn = attend(query_block, new_kv, kv_pool, page_counts[0], last_fill[0], page_order[0])
     partial_terms = jnp.dot(attn, out_weight, preferred_element_type=jnp.float32)
-    summed = lax.psum(partial_terms, "heads")
+    summed = partial_terms
+    for hop in (1, 2):
+        summed = summed + lax.ppermute(summed, "heads", [(dev, dev ^ hop) for dev in range(4)])
     mixed = hidden.astype(jnp.float32) + summed
     mean_square = jnp.mean(mixed * mixed, axis=1, keepdims=True)
     normed = (mixed * lax.rsqrt(mean_square + norm_epsilon) * norm_gain.astype(jnp.float32)).astype(

time: 97.1 us -> 90.5 us (0.932)
  between operations: 14.2 us -> 0.79 us
  waiting for transfers between devices: 41.5 us -> 48.2 us
  starting transfers between devices: 6.38 us -> 9.42 us
  other arithmetic: 6.9 us -> 4.89 us
    psum x1 -> x0, waiting for transfers between devices: 41.5 us -> none  [per_device(): summed = lax.psum(partial_terms, 'heads')]
    ppermute x0 -> x2, waiting for transfers between devices: none -> 39 us  [per_device(): lax.ppermute(summed, 'heads', [(dev, dev ^ hop) for dev in range(4)])]
    all_to_all x1, waiting for transfers between devices: 0.01 us -> 9.19 us  [per_device(): lax.all_to_all(outgoing, 'heads', split_axis=1, concat_axis=1, tiled=True)]
    ppermute x0 -> x2, starting transfers between devices: none -> 5.91 us  [per_device(): lax.ppermute(summed, 'heads', [(dev, dev ^ hop) for dev in range(4)])]
    all_to_all x1, starting transfers between devices: 6.35 us -> 3.52 us  [per_device(): lax.all_to_all(outgoing, 'heads', split_axis=1, concat_axis=1, tiled=True)]
    convert_element_type x1, other arithmetic: 1.89 us -> 0.84 us  [per_device(): (mixed * lax.rsqrt(mean_square + norm_epsilon) * norm_gain.astype(jnp.flo...]
    reduce_sum x1, other arithmetic: 1.22 us -> 0.2 us  [per_device(): mean_square = jnp.mean(mixed * mixed, axis=1, keepdims=True)]
  transfers between devices with their start and end apart: 2 -> 3, of which waited for: 1 -> 3; matrix products, arithmetic and copies ran while one was open for 7% -> 6% of each run, Pallas kernels for 0% -> 0%
where the time goes in v1:
time: 90.5 us; the launch traced here: 90.1 us
  waiting for transfers between devices  48.2 us (53%)
  matrix products  20.4 us (23%)
  starting transfers between devices  9.42 us (10%)
  local copies, waits for them, and re-layouts  6.41 us (7%)
  other arithmetic  4.89 us (5%)
    ppermute x2, waiting for transfers between devices, per_device(): lax.ppermute(summed, 'heads', [(dev, dev ^ hop) for dev in range(4)])  39 us
    dot_general x1, matrix products, per_device(): jnp.dot(attn, out_weight, preferred_element_type=jnp.float32)  12.8 us
    all_to_all x1, waiting for transfers between devices, per_device(): lax.all_to_all(outgoing, 'heads', split_axis=1, concat_axis=1, tiled=True)  9.19 us
    ppermute x2, starting transfers between devices, per_device(): lax.ppermute(summed, 'heads', [(dev, dev ^ hop) for dev in range(4)])  5.91 us
    dot_general x1, matrix products, attend(): jnp.einsum('lpgd,lptd->lpgt', page_queries, kv_pool[..., :head_dim], pref...  3.69 us
    all_to_all x1, starting transfers between devices, per_device(): lax.all_to_all(outgoing, 'heads', split_axis=1, concat_axis=1, tiled=True)  3.52 us
    dot_general x1, matrix products, attend(): jnp.einsum('lpgt,lptd->lpgd', weight.astype(jnp.bfloat16), kv_pool[..., h...  2.86 us
    unnamed x10, local copies, waits for them, and re-layouts  1.91 us
  transfers between devices with their start and end apart: 3, of which 3 were waited for; matrix products, arithmetic and copies ran while one was open for 6% of the time, Pallas kernels for 0%

profile of v1, /device:TPU:0, one launch (start us, length us, event | category | flops | bytes accessed | tf_op | source)
XLA Modules:
  0.0 90.1 jit_solution(973475816363750958)
XLA Ops:
  0.6 0.8 select_reduce_fusion.1
  1.5 0.7 copy.69
  2.2 0.1 reduce
  2.4 0.1 convert_reduce_fusion
  2.5 0.7 add_bitcast_fusion
  3.1 0.1 select_reduce_fusion.3
  3.2 0.7 convert_bitcast_fusion
  4.0 0.8 copy.93
  4.8 0.3 fusion.10
  5.1 0.1 fusion.26
  5.2 0.1 copy.90
  5.3 0.1 add_compare_fusion
  5.4 3.7 %fusion.47 = (f32[2,48,8]{2,1,0:T(8,128)S(1)}, f32[2,48,8,128]{3,2,1,0:T(8,128)S(1)}) fusion(bf16[2,48,128,256]{3,2,1,0:T(8,128)(2,1)} %param.13, bf16[2,48,8,128]{3,1,2,0:T(8,128)(2,1)S(1)} %fusion.10, pred[48,128]{1,0:T(8,128)(4,1)S(1)} %add_compare_fusion), kind=kOutput, calls=%fused_computation.85 | convolution fusion | flops 25459968 | bytes 3744768 | tf_op jit(solution)/shard_map/lpgd,lptd->lpgt/dot_general | solution.py:38
  9.1 0.1 copy.72
  9.1 0.1 select_reduce_fusion
  9.3 0.1 copy.73
  9.4 0.1 convolution_bitcast_fusion.1
  9.5 0.1 copy.74
  9.6 0.3 fusion.15
  9.9 2.9 %fusion = f32[2,48,8,128]{3,2,1,0:T(8,128)S(1)} fusion(bf16[2,48,128,256]{3,2,1,0:T(8,128)(2,1)} %param.13, f32[2,48,8,128]{3,2,1,0:T(8,128)S(1)} %get-tuple-element.26, f32[2,48,8]{2,1,0:T(8,128)S(1)} %copy.74, pred[48,128]{1,0:T(8,128)(4,1)S(1)} %add_compare_fusion), kind=kOutput, calls=%fused_computation.3 | convolution fusion | flops 25460736 | bytes 3941376 | tf_op jit(solution)/shard_map/lpgt,lptd->lpgd/dot_general | solution.py:59
  12.8 0.1 copy.76
  12.9 0.1 fusion.13
  13.0 0.3 fusion.12
  13.3 12.8 %fusion.22 = f32[16,8192]{1,0:T(8,128)S(1)} fusion(bf16[2048,8192]{1,0:T(8,128)(2,1)} %param.18, bf16[2,8,16,128]{3,2,1,0:T(8,128)(2,1)S(1)} %bitcast.73), kind=kOutput, calls=%fused_computation.30 | convolution fusion | flops 536870912 | bytes 34144256 | tf_op jit(solution)/shard_map/dot_general | solution.py:131
  26.2 3.1 %collective-permute-start = (f32[16,8192]{1,0:T(8,128)S(1)}, f32[16,8192]{1,0:T(8,128)S(1)}, u32[]{:S(2)}, u32[]{:S(2)}) collective-permute-start(f32[16,8192]{1,0:T(8,128)S(1)} %fusion.22), channel_id=1, source_target_pairs={{0,4},{4,0},{8,12},{12,8},{1,5},{5,1},{9,13},{13,9},{2,6},{6,2},{1... | collective-permute-start | bytes 1572872 | tf_op jit(solution)/shard_map/ppermute | solution.py:134
  29.3 0.2 convert_reduce_fusion.1
  29.5 0.1 reshape.257
  29.6 0.1 and_reduce_fusion
  29.7 0.1 copy.79
  29.8 0.2 fusion.29
  30.0 0.1 copy.82
  30.1 0.6 gather_fusion.1
  30.6 0.6 gather_fusion
  31.2 0.1 copy.92
  31.3 9.9 %collective-permute-done = f32[16,8192]{1,0:T(8,128)S(1)} collective-permute-done((f32[16,8192]{1,0:T(8,128)S(1)}, f32[16,8192]{1,0:T(8,128)S(1)}, u32[]{:S(2)}, u32[]{:S(2)}) %collective-permute-start) | collective-permute-done | bytes 524320 | tf_op jit(solution)/shard_map/ppermute | solution.py:134
  41.2 0.1 add.111
  41.2 2.8 %collective-permute-start.1 = (f32[16,8192]{1,0:T(8,128)S(1)}, f32[16,8192]{1,0:T(8,128)S(1)}, u32[]{:S(2)}, u32[]{:S(2)}) collective-permute-start(f32[16,8192]{1,0:T(8,128)S(1)} %add.111), channel_id=1, source_target_pairs={{0,8},{4,12},{8,0},{12,4},{1,9},{5,13},{9,1},{13,5},{2,10},{6,14},... | collective-permute-start | bytes 1572872 | tf_op jit(solution)/shard_map/ppermute | solution.py:134
  44.1 0.1 copy.84
  44.2 0.1 reshape.273
  44.3 0.6 gather_fusion.2
  44.9 0.1 broadcast_select_fusion
  45.0 1.1 %copy.85 = bf16[2,4,2,128,256]{4,3,2,0,1:T(8,128)(2,1)} copy(bf16[2,4,2,128,256]{4,3,2,1,0:T(8,128)(2,1)S(1)} %broadcast_select_fusion) | data formatting | bytes 2097152 | tf_op jit(solution)/shard_map/jit(_where)/select_n | solution.py:126
  46.1 3.5 %all-to-all-start = ((bf16[2,4,2,128,256]{4,3,2,0,1:T(8,128)(2,1)}), bf16[2,4,2,128,256]{4,3,2,0,1:T(8,128)(2,1)S(1)}, u32[]{:S(2)}, u32[]{:S(2)}) async-start(bf16[2,4,2,128,256]{4,3,2,0,1:T(8,128)(2,1)} %copy.85), calls=%async_computation | async-start | bytes 2097152 | tf_op jit(solution)/shard_map/all_to_all | solution.py:127
  49.7 29.1 %collective-permute-done.1 = f32[16,8192]{1,0:T(8,128)S(1)} collective-permute-done((f32[16,8192]{1,0:T(8,128)S(1)}, f32[16,8192]{1,0:T(8,128)S(1)}, u32[]{:S(2)}, u32[]{:S(2)}) %collective-permute-start.1) | collective-permute-done | bytes 524320 | tf_op jit(solution)/shard_map/ppermute | solution.py:134
  78.8 0.2 multiply_reduce_fusion
  79.0 0.8 multiply_convert_fusion
  79.9 9.2 %all-to-all-done = bf16[2,4,2,128,256]{4,3,2,0,1:T(8,128)(2,1)S(1)} async-done(((bf16[2,4,2,128,256]{4,3,2,0,1:T(8,128)(2,1)}), bf16[2,4,2,128,256]{4,3,2,0,1:T(8,128)(2,1)S(1)}, u32[]{:S(2)}, u32[]{:S(2)}) %all-to-all-start) | async-done | bytes 1048608 | tf_op jit(solution)/shard_map/all_to_all | solution.py:127
  89.1 1.0 %copy.86 = bf16[2,1,4,2,128,256]{5,4,3,2,1,0:T(8,128)(2,1)} copy(bf16[2,1,4,2,128,256]{5,4,3,0,2,1:T(8,128)(2,1)S(1)} %bitcast.71) | data formatting | bytes 2097152
  (23 shorter events, 0.2 us)
Async XLA Ops:
  0.6 43.6 %copy-start = (bf16[1,1,8,128,256]{4,3,2,1,0:T(8,128)(2,1)S(1)}, bf16[1,1,8,128,256]{4,3,2,1,0:T(8,128)(2,1)}, u32[]{:S(2)}) copy-start(bf16[1,1,8,128,256]{4,3,2,1,0:T(8,128)(2,1)} %param.20) | copy-start | bytes 1572868
  13.3 15.9 %copy-start.3 = (s32[1,1,8,1]{2,3,1,0:T(1,128)S(1)}, s32[1,1,8,1]{2,3,1,0:T(1,128)}, u32[]{:S(2)}) copy-start(s32[1,1,8,1]{2,3,1,0:T(1,128)} %param.21) | copy-start | bytes 100
  26.2 23.5 %copy-start.2 = (bf16[8192]{0:T(1024)(128)(2,1)S(1)}, bf16[8192]{0:T(1024)(128)(2,1)}, u32[]{:S(2)}) copy-start(bf16[8192]{0:T(1024)(128)(2,1)} %param.19) | copy-start | bytes 49156
  26.2 52.6 %copy-start.1 = (bf16[16,8192]{1,0:T(8,128)(2,1)S(1)}, bf16[16,8192]{1,0:T(8,128)(2,1)}, u32[]{:S(2)}) copy-start(bf16[16,8192]{1,0:T(8,128)(2,1)} %param.17) | copy-start | bytes 786436
  26.2 15.0 %collective-permute-start = (f32[16,8192]{1,0:T(8,128)S(1)}, f32[16,8192]{1,0:T(8,128)S(1)}, u32[]{:S(2)}, u32[]{:S(2)}) collective-permute-start(f32[16,8192]{1,0:T(8,128)S(1)} %fusion.22), channel_id=1, source_target_pairs={{0,4},{4,0},{8,12},{12,8},{1,5},{5,1},{9,13},{13,9},{2,6},{6,2},{1... | collective-permute-start | bytes 1572872 | tf_op jit(solution)/shard_map/ppermute | solution.py:134
  41.2 37.6 %collective-permute-start.1 = (f32[16,8192]{1,0:T(8,128)S(1)}, f32[16,8192]{1,0:T(8,128)S(1)}, u32[]{:S(2)}, u32[]{:S(2)}) collective-permute-start(f32[16,8192]{1,0:T(8,128)S(1)} %add.111), channel_id=1, source_target_pairs={{0,8},{4,12},{8,0},{12,4},{1,9},{5,13},{9,1},{13,5},{2,10},{6,14},... | collective-permute-start | bytes 1572872 | tf_op jit(solution)/shard_map/ppermute | solution.py:134
  46.1 42.9 %all-to-all-start = ((bf16[2,4,2,128,256]{4,3,2,0,1:T(8,128)(2,1)}), bf16[2,4,2,128,256]{4,3,2,0,1:T(8,128)(2,1)S(1)}, u32[]{:S(2)}, u32[]{:S(2)}) async-start(bf16[2,4,2,128,256]{4,3,2,0,1:T(8,128)(2,1)} %copy.85), calls=%async_computation | async-start | bytes 2097152 | tf_op jit(solution)/shard_map/all_to_all | solution.py:127
